TPU v7x, 8 devices: a whole 2x2x1 slice. The times are simulated.
8 devices in a mesh: dp: 1 (over z), tp: 2 (over y), cp: 4 (over x, core).
Axes of the slice: x: 2, y: 2, z: 1, core: 2. Of those that a mesh axis runs over, the one named last changes fastest.
Arguments:
- x: bfloat16 [4096, 4096], P(('dp', 'cp'))
- kc: bfloat16 [8192, 32, 128], P(('dp', 'cp'), 'tp')
- vc: bfloat16 [8192, 32, 128], P(('dp', 'cp'), 'tp')
- wq: bfloat16 [4096, 4096], P(None, 'tp')
- wk: bfloat16 [4096, 4096], P(None, 'tp')
- wv: bfloat16 [4096, 4096], P(None, 'tp')
- wo: bfloat16 [4096, 4096], P('tp')
Outputs:
- output 1: bfloat16 [4096, 4096], P(('dp', 'cp'), 'tp')
- output 2: bfloat16 [4096, 32, 128], P(('dp', 'cp'), 'tp')
- output 3: bfloat16 [4096, 32, 128], P(('dp', 'cp'), 'tp')
All inputs are finite; a program needn't handle non-finite values.
Results may differ from a plain program's by a relative error of at most 0.011.
Values are sent between devices in bfloat16 or wider.
A program may use at most 1 GiB of HBM per device.

v0:
```python
import jax
import jax.numpy as jnp
from jax import lax
from jax.sharding import PartitionSpec as P

THETA = 500000.0


def _rope(a, pos):
    d = a.shape[-1]
    half = d // 2
    inv = 1.0 / (THETA ** (jnp.arange(half, dtype=jnp.float32) * 2.0 / d))
    ang = pos.astype(jnp.float32)[:, None] * inv[None, :]
    cos = jnp.cos(ang)[:, None, :]
    sin = jnp.sin(ang)[:, None, :]
    af = a.astype(jnp.float32)
    a1 = af[..., :half]
    a2 = af[..., half:]
    return jnp.concatenate([a1 * cos - a2 * sin, a2 * cos + a1 * sin], axis=-1).astype(jnp.bfloat16)


def _project(x, w, n, d):
    return jnp.dot(x, w, preferred_element_type=jnp.float32).astype(jnp.bfloat16).reshape(x.shape[0], n, d)


def _attend(q, k, v, mask):
    s = jnp.einsum('pjif,ojf->pjio', q, k, preferred_element_type=jnp.float32) * (q.shape[-1] ** -0.5)
    if mask is not None:
        s = jnp.where(mask[:, None, None, :], s, -jnp.inf)
    mx = jnp.max(s, axis=-1)
    p = jnp.exp(s - mx[..., None])
    l = jnp.sum(p, axis=-1)
    o = jnp.einsum('pjio,ojf->pjif', p.astype(jnp.bfloat16), v, preferred_element_type=jnp.float32)
    return o / l[..., None], mx + jnp.log(l)


def _merge(o1, l1, o2, l2):
    m = jnp.maximum(l1, l2)
    w1 = jnp.exp(l1 - m)
    w2 = jnp.exp(l2 - m)
    tot = w1 + w2
    return (o1 * w1[..., None] + o2 * w2[..., None]) / tot[..., None], m + jnp.log(tot)


def solution(mesh):
    ncp = mesh.shape['cp']
    row = P(('dp', 'cp'), None)
    cache = P(('dp', 'cp'), 'tp', None)
    col = P(None, 'tp')
    perm = [(i, (i + 1) % ncp) for i in range(ncp)]

    def body(x, kc, vc, wq, wk, wv, wo):
        tl = x.shape[0]
        cl, hkvl, d = kc.shape
        hl = wq.shape[1] // d
        g = hl // hkvl
        r = lax.axis_index('cp')
        pos = cl * ncp + r * tl + jnp.arange(tl, dtype=jnp.int32)
        q = _rope(_project(x, wq, hl, d), pos).reshape(tl, hkvl, g, d)
        k = _rope(_project(x, wk, hkvl, d), pos)
        v = _project(x, wv, hkvl, d)
        k_all = lax.all_gather(k, 'cp', axis=0, tiled=True)
        v_all = lax.all_gather(v, 'cp', axis=0, tiled=True)
        mask = jnp.arange(tl * ncp)[None, :] <= (r * tl + jnp.arange(tl))[:, None]
        o, lse = _attend(q, k_all, v_all, mask)
        kb, vb = kc, vc
        for step in range(ncp):
            if step > 0:
                kb = lax.ppermute(kb, 'cp', perm)
                vb = lax.ppermute(vb, 'cp', perm)
            ob, lb = _attend(q, kb, vb, None)
            o, lse = _merge(o, lse, ob, lb)
        yp = jnp.dot(o.reshape(tl, hl * d).astype(jnp.bfloat16), wo, preferred_element_type=jnp.float32)
        y = lax.psum_scatter(yp, 'tp', scatter_dimension=1, tiled=True).astype(jnp.bfloat16)
        return y, k, v

    return jax.shard_map(body, mesh=mesh,
                         in_specs=(row, cache, cache, col, col, col, P('tp', None)),
                         out_specs=(P(('dp', 'cp'), 'tp'), cache, cache), check_vma=False)
```

profile of v0, /device:TPU:0, one launch (start us, length us, event | category | flops | bytes accessed | tf_op | source)
XLA Modules:
  0.0 1398.6 jit_solution(11156918326238490994)
XLA Ops:
  7.2 21.4 %convert_bitcast_fusion = f32[128,8,16,128]{3,1,2,0:T(8,128)S(1)} fusion(bf16[1024,4096]{1,0:T(8,128)(2,1)} %param.7, bf16[4096,2048]{1,0:T(8,128)(2,1)} %param.10), kind=kOutput, calls=%fused_computation.55 | convolution fusion | flops 17184063488 | bytes 33554432 | tf_op jit(solution)/shard_map/dot_general | solution.py:23
  30.7 21.9 %convert_bitcast_fusion.1 = f32[128,8,16,128]{3,1,2,0:T(8,128)S(1)} fusion(bf16[1024,4096]{1,0:T(8,128)(2,1)} %param.7, bf16[4096,2048]{1,0:T(8,128)(2,1)} %param.11), kind=kOutput, calls=%fused_computation.56 | convolution fusion | flops 17184063488 | bytes 33554432 | tf_op jit(solution)/shard_map/dot_general | solution.py:23
  78.2 25.3 %subtract_convert_fusion.1 = (bf16[1024,16,64]{2,0,1:T(8,128)(2,1)S(1)}, bf16[1024,16,64]{2,0,1:T(8,128)(2,1)S(1)}, bf16[1024,16,64]{2,0,1:T(8,128)(2,1)}, bf16[1024,16,64]{2,0,1:T(8,128)(2,1)}) fusion(f32[1024,16,64]{2,1,0:T(8,128)} %get-tuple-element.22, f32[1024,16,64]{2,1,0:T(8,128)} %get-tuple-element.21, f32[1024,64]{1,0:T(8,128)S(1)} %get-tuple-element.37, ...), kind=kLoop, calls=%fused_computation.60 | loop fusion | flops 16777216 | bytes 25690112 | tf_op jit(solution)/shard_map/convert.4
  132.2 22.7 %convert_bitcast_fusion.2 = bf16[128,8,16,128]{3,1,2,0:T(8,128)(2,1)S(1)} fusion(bf16[1024,4096]{1,0:T(8,128)(2,1)} %param.7, bf16[4096,2048]{1,0:T(8,128)(2,1)} %param.12), kind=kOutput, calls=%fused_computation.64 | convolution fusion | flops 17181966336 | bytes 29360128 | tf_op jit(solution)/shard_map/dot_general | solution.py:23
  171.0 48.0 %bitcast_reduce_fusion.3 = (f32[1024,16]{0,1:T(8,128)S(1)}, f32[16,1024,2048]{2,1,0:T(8,128)}) fusion(bf16[1024,16,128]{2,0,1:T(8,128)(2,1)} %pad_maximum_fusion.1, bf16[2048,16,128]{2,1,0:T(8,128)(2,1)} %param.8), kind=kOutput, calls=%fused_computation.16 | convolution fusion | flops 8657027072 | bytes 146866176 | tf_op jit(solution)/shard_map/pjif,ojf->pjio/dot_general | solution.py:27
  219.1 41.7 %fusion.12 = f32[1024,16]{0,1:T(8,128)} fusion(f32[16,1024,2048]{2,1,0:T(8,128)} %get-tuple-element.43, f32[1024,16]{0,1:T(8,128)S(1)} %get-tuple-element.42), kind=kLoop, calls=%fused_computation.21 | loop fusion | flops 100646912 | bytes 134348800 | tf_op jit(solution)/shard_map/reduce_sum | solution.py:32
  260.8 48.8 %fusion.23 = f32[16,1024,128]{1,2,0:T(8,128)} fusion(bf16[2048,16,128]{0,2,1:T(8,128)(2,1)} %copy.17, f32[16,1024,2048]{2,1,0:T(8,128)} %get-tuple-element.43, f32[1024,16]{0,1:T(8,128)S(1)} %get-tuple-element.42), kind=kOutput, calls=%fused_computation.32 | convolution fusion | flops 8690597888 | bytes 151060480 | tf_op jit(solution)/shard_map/pjio,ojf->pjif/dot_general | solution.py:33
  315.3 37.0 %collective-permute-done = bf16[2048,16,128]{2,0,1:T(8,128)(2,1)} collective-permute-done((bf16[2048,16,128]{2,0,1:T(8,128)(2,1)}, bf16[2048,16,128]{2,0,1:T(8,128)(2,1)}, u32[]{:S(2)}, u32[]{:S(2)}) %collective-permute-start) | collective-permute-done | bytes 8388640 | tf_op jit(solution)/shard_map/ppermute | solution.py:69
  356.3 48.2 %bitcast_reduce_fusion.2 = (f32[1024,16]{0,1:T(8,128)S(1)}, f32[16,1024,2048]{2,1,0:T(8,128)}) fusion(bf16[1024,16,128]{2,0,1:T(8,128)(2,1)} %pad_maximum_fusion.1, bf16[2048,16,128]{2,0,1:T(8,128)(2,1)} %collective-permute-done), kind=kOutput, calls=%fused_computation.13 | convolution fusion | flops 8657027072 | bytes 146866176 | tf_op jit(solution)/shard_map/pjif,ojf->pjio/dot_general | solution.py:27
  404.5 75.0 %collective-permute-done.1 = bf16[2048,16,128]{0,2,1:T(8,128)(2,1)} collective-permute-done((bf16[2048,16,128]{0,2,1:T(8,128)(2,1)}, bf16[2048,16,128]{0,2,1:T(8,128)(2,1)}, u32[]{:S(2)}, u32[]{:S(2)}) %collective-permute-start.1) | collective-permute-done | bytes 8388640 | tf_op jit(solution)/shard_map/ppermute | solution.py:70
  479.5 48.8 %fusion.25 = f32[16,1024,128]{1,2,0:T(8,128)} fusion(bf16[2048,16,128]{0,2,1:T(8,128)(2,1)} %collective-permute-done.1, f32[16,1024,2048]{2,1,0:T(8,128)} %get-tuple-element.41, f32[1024,16]{0,1:T(8,128)S(1)} %get-tuple-element.40), kind=kOutput, calls=%fused_computation.33 | convolution fusion | flops 8690597888 | bytes 151060480 | tf_op jit(solution)/shard_map/pjio,ojf->pjif/dot_general | solution.py:33
  528.3 41.7 %fusion.14 = f32[1024,16]{0,1:T(8,128)} fusion(f32[16,1024,2048]{2,1,0:T(8,128)} %get-tuple-element.41, f32[1024,16]{0,1:T(8,128)S(1)} %get-tuple-element.40), kind=kLoop, calls=%fused_computation.23 | loop fusion | flops 100646912 | bytes 134348800 | tf_op jit(solution)/shard_map/reduce_sum | solution.py:32
  572.4 48.0 %bitcast_reduce_fusion.1 = (f32[1024,16]{0,1:T(8,128)S(1)}, f32[16,1024,2048]{2,1,0:T(8,128)}) fusion(bf16[1024,16,128]{2,0,1:T(8,128)(2,1)} %pad_maximum_fusion.1, bf16[2048,16,128]{2,0,1:T(8,128)(2,1)} %collective-permute-done.2), kind=kOutput, calls=%fused_computation.10 | convolution fusion | flops 8657027072 | bytes 146866176 | tf_op jit(solution)/shard_map/pjif,ojf->pjio/dot_general | solution.py:27
  620.4 41.7 %fusion.16 = f32[1024,16]{0,1:T(8,128)} fusion(f32[16,1024,2048]{2,1,0:T(8,128)} %get-tuple-element.39, f32[1024,16]{0,1:T(8,128)S(1)} %get-tuple-element.38), kind=kLoop, calls=%fused_computation.25 | loop fusion | flops 100646912 | bytes 134348800 | tf_op jit(solution)/shard_map/reduce_sum | solution.py:32
  662.1 49.0 %fusion.27 = f32[16,1024,128]{1,2,0:T(8,128)} fusion(bf16[2048,16,128]{0,2,1:T(8,128)(2,1)} %collective-permute-done.3, f32[16,1024,2048]{2,1,0:T(8,128)} %get-tuple-element.39, f32[1024,16]{0,1:T(8,128)S(1)} %get-tuple-element.38), kind=kOutput, calls=%fused_computation.34 | convolution fusion | flops 8690597888 | bytes 151060480 | tf_op jit(solution)/shard_map/pjio,ojf->pjif/dot_general | solution.py:33
  711.2 38.0 %collective-permute-done.4 = bf16[2048,16,128]{2,0,1:T(8,128)(2,1)} collective-permute-done((bf16[2048,16,128]{2,0,1:T(8,128)(2,1)}, bf16[2048,16,128]{2,0,1:T(8,128)(2,1)}, u32[]{:S(2)}, u32[]{:S(2)}) %collective-permute-start.4) | collective-permute-done | bytes 8388640 | tf_op jit(solution)/shard_map/ppermute | solution.py:69
  749.2 48.0 %bitcast_reduce_fusion = (f32[1024,16]{0,1:T(8,128)S(1)}, f32[16,1024,2048]{2,1,0:T(8,128)}) fusion(bf16[1024,16,128]{2,0,1:T(8,128)(2,1)} %pad_maximum_fusion.1, bf16[2048,16,128]{2,0,1:T(8,128)(2,1)} %collective-permute-done.4), kind=kOutput, calls=%fused_computation.7 | convolution fusion | flops 8657027072 | bytes 146866176 | tf_op jit(solution)/shard_map/pjif,ojf->pjio/dot_general | solution.py:27
  797.2 41.7 %fusion.18 = f32[1024,16]{0,1:T(8,128)} fusion(f32[16,1024,2048]{2,1,0:T(8,128)} %get-tuple-element.47, f32[1024,16]{0,1:T(8,128)S(1)} %get-tuple-element.46), kind=kLoop, calls=%fused_computation.27 | loop fusion | flops 100646912 | bytes 134348800 | tf_op jit(solution)/shard_map/reduce_sum | solution.py:32
  838.9 97.5 %fusion.2 = (f32[1024,16]{0,1:T(8,128)S(1)}, f32[16,4096,1024]{2,1,0:T(8,128)}) fusion(pred[1024,4096]{0,1:T(8,128)(4,1)} %iota_compare_fusion, bf16[4096,16,128]{2,0,1:T(8,128)(2,1)} %all-gather.5.cloned.1.call-done, bf16[1024,16,128]{2,0,1:T(8,128)(2,1)} %pad_maximum_fusion.1), kind=kOutput, calls=%fused_computation.4 | convolution fusion | flops 17381179392 | bytes 293666816 | tf_op jit(solution)/shard_map/pjif,ojf->pjio/dot_general | solution.py:27
  936.4 96.2 %fusion.8 = f32[16,128,1024]{2,1,0:T(8,128)} fusion(bf16[4096,16,128]{0,2,1:T(8,128)(2,1)} %all-gather.3.cloned.1.call-done, f32[16,4096,1024]{2,1,0:T(8,128)} %get-tuple-element.45, f32[1024,16]{0,1:T(8,128)S(1)} %get-tuple-element.44, pred[1024,4096]{0,1:T(8,128)(4,1)} %iota_compare_fusion), kind=kOutput, calls=%fused_computation.18 | convolution fusion | flops 17448304640 | bytes 297861120 | tf_op jit(solution)/shard_map/pjio,ojf->pjif/dot_general | solution.py:33
  1032.6 81.9 %fusion = f32[1024,16]{0,1:T(8,128)S(1)} fusion(f32[16,4096,1024]{2,1,0:T(8,128)} %get-tuple-element.45, f32[1024,16]{0,1:T(8,128)S(1)} %get-tuple-element.44, pred[1024,4096]{0,1:T(8,128)(4,1)} %iota_compare_fusion), kind=kLoop, calls=%fused_computation.2 | loop fusion | flops 268419072 | bytes 272760832 | tf_op jit(solution)/shard_map/reduce_sum | solution.py:32
  1114.9 58.3 %fusion.44 = bf16[1024,16,1,128]{0,3,1,2:T(8,128)(2,1)} fusion(f32[16,1024,128]{1,2,0:T(8,128)} %fusion.27, f32[16,1024,128]{1,2,0:T(8,128)} %fusion.25, f32[16,1024,128]{1,2,0:T(8,128)} %fusion.23, f32[16,128,1024]{2,1,0:T(8,128)} %fusion.8, f32[1024,16]{0,1:T(8,128)S(1)} %get-tuple-element.28, f32[1024,16]{0,1:T(8,128)S(1)} %get-tuple-element.27, ...), kind=kOutput, calls=%fused_computation.61 | convolution fusion | flops 8736735232 | bytes 181534720 | tf_op jit(solution)/shard_map/pjio,ojf->pjif/dot_general | solution.py:33
  1173.2 24.0 %fusion.66 = f32[1024,4096]{1,0:T(8,128)} fusion(bf16[1024,2048]{0,1:T(8,128)(2,1)} %bitcast.216, bf16[2048,4096]{1,0:T(8,128)(2,1)} %param.13), kind=kOutput, calls=%fused_computation.103 | convolution fusion | flops 17179869184 | bytes 37748736 | tf_op jit(solution)/shard_map/dot_general | solution.py:73
  1204.1 181.4 %reduce-scatter.2.cloned.1.call-done = f32[1024,2048]{1,0:T(8,128)} async-done(((f32[1024,4096]{1,0:T(8,128)}), f32[1024,2048]{1,0:T(8,128)}) %reduce-scatter.2.cloned.1.call-update) | async-done | bytes 8388624 | tf_op jit(solution)/shard_map/reduce_scatter | solution.py:74
  (60 shorter events, 97.9 us)
Async XLA Ops:
  7.2 831.7 %all-gather.5.cloned.1.call-start = ((), (), s32[]{:S(2)}) async-start(), calls=%async_computation.2 | async-start | bytes 20971520 | tf_op jit(solution)/shard_map/all_gather | solution.py:62
  107.1 829.3 %all-gather.3.cloned.1.call-start = ((), (), s32[]{:S(2)}) async-start(), calls=%async_computation.1 | async-start | bytes 20971520 | tf_op jit(solution)/shard_map/all_gather | solution.py:63
  116.0 236.4 %collective-permute-start = (bf16[2048,16,128]{2,0,1:T(8,128)(2,1)}, bf16[2048,16,128]{2,0,1:T(8,128)(2,1)}, u32[]{:S(2)}, u32[]{:S(2)}) collective-permute-start(bf16[2048,16,128]{2,0,1:T(8,128)(2,1)} %copy.16), channel_id=1, source_target_pairs={{0,1},{1,2},{2,3},{3,0},{4,5},{5,6},{6,7},{7,4}} | collective-permute-start | bytes 25165832 | tf_op jit(solution)/shard_map/ppermute | solution.py:69
  129.6 349.9 %collective-permute-start.1 = (bf16[2048,16,128]{0,2,1:T(8,128)(2,1)}, bf16[2048,16,128]{0,2,1:T(8,128)(2,1)}, u32[]{:S(2)}, u32[]{:S(2)}) collective-permute-start(bf16[2048,16,128]{0,2,1:T(8,128)(2,1)} %copy.17), channel_id=1, source_target_pairs={{0,1},{1,2},{2,3},{3,0},{4,5},{5,6},{6,7},{7,4}} | collective-permute-start | bytes 25165832 | tf_op jit(solution)/shard_map/ppermute | solution.py:70
  165.0 1220.5 %reduce-scatter.2.cloned.1.call-start = ((), (), s32[]{:S(2)}) async-start(), calls=%async_computation.3 | async-start | bytes 25165824 | tf_op jit(solution)/shard_map/reduce_scatter | solution.py:74
  219.1 41.7 %copy-start.4 = (f32[1024,16]{0,1:T(8,128)}, f32[1024,16]{0,1:T(8,128)S(1)}, u32[]{:S(2)}) copy-start(f32[1024,16]{0,1:T(8,128)S(1)} %get-tuple-element.42) | copy-start | bytes 196612
  352.3 217.6 %collective-permute-start.2 = (bf16[2048,16,128]{2,0,1:T(8,128)(2,1)}, bf16[2048,16,128]{2,0,1:T(8,128)(2,1)}, u32[]{:S(2)}, u32[]{:S(2)}) collective-permute-start(bf16[2048,16,128]{2,0,1:T(8,128)(2,1)} %collective-permute-done), channel_id=1, source_target_pairs={{0,1},{1,2},{2,3},{3,0},{4,5},{5,6},{6,7},{7,4}} | collective-permute-start | bytes 25165832 | tf_op jit(solution)/shard_map/ppermute | solution.py:69
  404.5 123.8 %copy-start.6 = (f32[1024,16]{0,1:T(8,128)}, f32[1024,16]{0,1:T(8,128)S(1)}, u32[]{:S(2)}) copy-start(f32[1024,16]{0,1:T(8,128)S(1)} %get-tuple-element.40) | copy-start | bytes 196612
  479.5 182.6 %collective-permute-start.3 = (bf16[2048,16,128]{0,2,1:T(8,128)(2,1)}, bf16[2048,16,128]{0,2,1:T(8,128)(2,1)}, u32[]{:S(2)}, u32[]{:S(2)}) collective-permute-start(bf16[2048,16,128]{0,2,1:T(8,128)(2,1)} %collective-permute-done.1), channel_id=1, source_target_pairs={{0,1},{1,2},{2,3},{3,0},{4,5},{5,6},{6,7},{7,4}} | collective-permute-start | bytes 25165832 | tf_op jit(solution)/shard_map/ppermute | solution.py:70
  569.9 179.2 %collective-permute-start.4 = (bf16[2048,16,128]{2,0,1:T(8,128)(2,1)}, bf16[2048,16,128]{2,0,1:T(8,128)(2,1)}, u32[]{:S(2)}, u32[]{:S(2)}) collective-permute-start(bf16[2048,16,128]{2,0,1:T(8,128)(2,1)} %collective-permute-done.2), channel_id=1, source_target_pairs={{0,1},{1,2},{2,3},{3,0},{4,5},{5,6},{6,7},{7,4}} | collective-permute-start | bytes 25165832 | tf_op jit(solution)/shard_map/ppermute | solution.py:69
  620.4 41.7 %copy-start.2 = (f32[1024,16]{0,1:T(8,128)}, f32[1024,16]{0,1:T(8,128)S(1)}, u32[]{:S(2)}) copy-start(f32[1024,16]{0,1:T(8,128)S(1)} %get-tuple-element.38) | copy-start | bytes 196612
  662.1 452.8 %collective-permute-start.5 = (bf16[2048,16,128]{0,2,1:T(8,128)(2,1)}, bf16[2048,16,128]{0,2,1:T(8,128)(2,1)}, u32[]{:S(2)}, u32[]{:S(2)}) collective-permute-start(bf16[2048,16,128]{0,2,1:T(8,128)(2,1)} %collective-permute-done.3), channel_id=1, source_target_pairs={{0,1},{1,2},{2,3},{3,0},{4,5},{5,6},{6,7},{7,4}} | collective-permute-start | bytes 25165832 | tf_op jit(solution)/shard_map/ppermute | solution.py:70
  797.2 41.7 %copy-start = (f32[1024,16]{0,1:T(8,128)}, f32[1024,16]{0,1:T(8,128)S(1)}, u32[]{:S(2)}) copy-start(f32[1024,16]{0,1:T(8,128)S(1)} %get-tuple-element.46) | copy-start | bytes 196612
  1032.6 81.9 %copy-start.5 = (f32[1024,16]{0,1:T(8,128)S(1)}, f32[1024,16]{0,1:T(8,128)}, u32[]{:S(2)}) copy-start(f32[1024,16]{0,1:T(8,128)} %copy-done.4) | copy-start | bytes 196612
  1032.6 81.9 %copy-start.7 = (f32[1024,16]{0,1:T(8,128)S(1)}, f32[1024,16]{0,1:T(8,128)}, u32[]{:S(2)}) copy-start(f32[1024,16]{0,1:T(8,128)} %copy-done.6) | copy-start | bytes 196612
  1032.6 82.0 %copy-start.10 = (f32[1024,16]{0,1:T(8,128)S(1)}, f32[1024,16]{0,1:T(8,128)}, u32[]{:S(2)}) copy-start(f32[1024,16]{0,1:T(8,128)} %fusion.12) | copy-start | bytes 196612
  1032.6 82.0 %copy-start.11 = (f32[1024,16]{0,1:T(8,128)S(1)}, f32[1024,16]{0,1:T(8,128)}, u32[]{:S(2)}) copy-start(f32[1024,16]{0,1:T(8,128)} %fusion.14) | copy-start | bytes 196612
  1032.6 82.1 %copy-start.1 = (f32[1024,16]{0,1:T(8,128)S(1)}, f32[1024,16]{0,1:T(8,128)}, u32[]{:S(2)}) copy-start(f32[1024,16]{0,1:T(8,128)} %copy-done) | copy-start | bytes 196612
  1032.6 82.1 %copy-start.3 = (f32[1024,16]{0,1:T(8,128)S(1)}, f32[1024,16]{0,1:T(8,128)}, u32[]{:S(2)}) copy-start(f32[1024,16]{0,1:T(8,128)} %copy-done.2) | copy-start | bytes 196612
  1032.6 82.1 %copy-start.8 = (f32[1024,16]{0,1:T(8,128)S(1)}, f32[1024,16]{0,1:T(8,128)}, u32[]{:S(2)}) copy-start(f32[1024,16]{0,1:T(8,128)} %fusion.18) | copy-start | bytes 196612
  1032.6 82.1 %copy-start.9 = (f32[1024,16]{0,1:T(8,128)S(1)}, f32[1024,16]{0,1:T(8,128)}, u32[]{:S(2)}) copy-start(f32[1024,16]{0,1:T(8,128)} %fusion.16) | copy-start | bytes 196612
Sparse Core Ops, SparseCore 0:
  107.2 152.2 all-gather.4
  261.0 149.3 all-gather.2
  1197.3 188.0 reduce-scatter.1
where the time goes:
time: 1410 us; the launch traced here: 1400 us
  matrix products  681 us (48%)
  waiting for transfers between devices  331 us (23%)
  other arithmetic  297 us (21%)
  local copies, waits for them, and re-layouts  64.2 us (5%)
  between operations  14.5 us (1%)
    dot_general x5, matrix products, _attend(): jnp.einsum('pjio,ojf->pjif', p.astype(jnp.bfloat16), v, preferred_element...  301 us
    dot_general x5, matrix products, _attend(): jnp.einsum('pjif,ojf->pjio', q, k, preferred_element_type=jnp.float32)  290 us
    reduce_sum x5, other arithmetic, _attend(): l = jnp.sum(p, axis=-1)  249 us
    reduce_scatter x1, waiting for transfers between devices, body(): lax.psum_scatter(yp, 'tp', scatter_dimension=1, tiled=True)  181 us
    ppermute x3, waiting for transfers between devices, body(): kb = lax.ppermute(kb, 'cp', perm)  75 us
    ppermute x3, waiting for transfers between devices, body(): vb = lax.ppermute(vb, 'cp', perm)  75 us
    dot_general x3, matrix products, _project(): jnp.dot(x, w, preferred_element_type=jnp.float32).astype(jnp.bfloat16)  66 us
    unnamed x30, local copies, waits for them, and re-layouts  39.2 us
  transfers between devices with their start and end apart: 9, of which 4 were waited for; matrix products, arithmetic and copies ran while one was open for 61% of the time, Pallas kernels for 0%

commit v1 on v0

v1 whole, which is shorter than its diff:
```python
import functools
import math

import jax
import jax.numpy as jnp
from jax import lax
from jax.experimental import pallas as pl
from jax.experimental.pallas import tpu as pltpu
from jax.sharding import PartitionSpec as P


THETA = 500000.0
F32 = jnp.float32
BF16 = jnp.bfloat16
NEG = -1e30
VMEM = 60 * 1024 * 1024
ORDER = (('R', 0, 4), ('R', 4, 4), ('L', 0, 8), ('R', 8, 4), ('R', 12, 4), ('M', 0, 8), ('L', 8, 8), ('M', 8, 4),
         ('M', 12, 4), ('Y', 0, 12), ('Z', 12, 4))


def _after(a, *deps):
    return lax.optimization_barrier((a, *deps))[0]


def _tables(pos, d):
    half = d // 2
    inv = 1.0 / (THETA ** (jnp.arange(half, dtype=F32) * 2.0 / d))
    ang = pos.astype(F32)[:, None] * inv[None, :]
    cos, sin = jnp.cos(ang), jnp.sin(ang)
    return jnp.concatenate([cos, cos], axis=1), jnp.concatenate([-sin, sin], axis=1)


def _proj(x, w, tabs, col0, ncols, d, bn=256):
    m, k = x.shape

    def kern(*refs):
        if tabs is None:
            x_ref, w_ref, o_ref = refs
        else:
            x_ref, w_ref, c_ref, s_ref, o_ref = refs
        r = jnp.dot(x_ref[...], w_ref[...], preferred_element_type=F32).astype(BF16)
        if tabs is None:
            o_ref[...] = r
        else:
            for h in range(bn // d):
                a = r[:, h * d:(h + 1) * d].astype(F32)
                o_ref[:, h * d:(h + 1) * d] = (a * c_ref[...] + pltpu.roll(a, d // 2, 1) * s_ref[...]).astype(BF16)

    full = lambda s: pl.BlockSpec(s, lambda j: (0, 0))
    j0 = col0 // bn
    extra = [] if tabs is None else [full((m, d)), full((m, d))]
    return pl.pallas_call(
        kern,
        grid=(ncols // bn,),
        in_specs=[full((m, k)), pl.BlockSpec((k, bn), lambda j: (0, j + j0))] + extra,
        out_specs=pl.BlockSpec((m, bn), lambda j: (0, j)),
        out_shape=jax.ShapeDtypeStruct((m, ncols), BF16),
        compiler_params=pltpu.CompilerParams(vmem_limit_bytes=VMEM),
        cost_estimate=pl.CostEstimate(flops=2 * m * k * ncols, bytes_accessed=2 * (m * k + k * ncols + m * ncols),
                                      transcendentals=0),
    )(x, w, *(tabs or ()))


def _attend(flags, q, qcol, kvs, h0, nh, d, causal):
    tq = q.shape[0]
    c = kvs[0][0].shape[0]
    n = kvs[2][0].shape[0]
    m0 = 64
    hq = tq // 2
    fb = 128
    scale = (d ** -0.5) * math.log2(math.e)
    tdot = lambda a, b: lax.dot_general(a, b, (((1,), (1,)), ((), ())), preferred_element_type=F32)
    vdot = lambda a, b: lax.dot_general(a, b, (((0,), (0,)), ((), ())), preferred_element_type=F32)

    def kern(f_ref, q_ref, *refs):
        ks, vs = refs[0:4], refs[4:8]
        o_ref, l_ref, acc_sc, d_sc = refs[8:]
        qf = q_ref[...].astype(F32) * scale
        hi = qf.astype(BF16)
        q2 = jnp.concatenate([hi, (qf - hi.astype(F32)).astype(BF16)], axis=1).T

        def scores(k_ref, row, rows, q0, qn):
            kb = k_ref[row:row + rows, :]
            return jnp.dot(jnp.concatenate([kb, kb], axis=1), q2[:, q0:q0 + qn], preferred_element_type=F32)

        mc = jnp.max(scores(ks[0], 0, m0, 0, tq), axis=0, keepdims=True)

        def run(parts, den, acc):
            for a, bk, q0, qn, masked in parts:
                s = scores(ks[a], 0, bk, q0, qn)
                if masked:
                    kp = lax.broadcasted_iota(jnp.int32, (bk, qn), 0)
                    qp = lax.broadcasted_iota(jnp.int32, (bk, qn), 1) + q0
                    s = jnp.where(kp <= qp, s, NEG)
                p = jnp.exp2(s - mc[:, q0:q0 + qn])
                den[q0, qn] = den.get((q0, qn), 0) + jnp.sum(p.reshape(bk // 8, 8, qn), axis=0)
                acc[q0, qn] = acc.get((q0, qn), 0) + vdot(vs[a][:bk, :], p.astype(BF16))

        def flush(parts, first):
            den, acc = {}, {}
            run(parts, den, acc)
            for i, (q0, qn) in enumerate(den):
                if first and i == 0:
                    d_sc[:, q0:q0 + qn] = den[q0, qn]
                    acc_sc[:, q0:q0 + qn] = acc[q0, qn]
                else:
                    d_sc[:, q0:q0 + qn] += den[q0, qn]
                    acc_sc[:, q0:q0 + qn] += acc[q0, qn]

        parts = [(0, c, 0, tq, False), (1, c, 0, tq, False)]
        if causal:
            parts += [(2, hq, 0, hq, True), (2, tq, hq, hq, True)]
        flush(parts, True)

        @pl.when(f_ref[1 if causal else 0] == 1)
        def _():
            flush([(a, n, 0, tq, False) for a in ((3,) if causal else (2, 3))], False)

        def finish(den, acc, m, qs):
            o_ref[:, qs] = acc / den
            l_ref[0, :, qs] = m + jnp.log2(den)

        den = jnp.sum(d_sc[...], axis=0, keepdims=True)
        top = jnp.max(jnp.abs(acc_sc[...]), axis=0, keepdims=True)
        good = jnp.where((den < 2.0 ** 100) & (top < 2.0 ** 126), 1.0, 0.0)
        finish(den, acc_sc[...], mc, slice(None))

        @pl.when(jnp.min(good) < 0.5)
        def _():
            def qblock(i, _):
                qs = pl.ds(pl.multiple_of(i * fb, fb), fb)
                qb = q_ref[qs, :]

                def kstep(k_ref, v_ref, masked):
                    def step(j, carry):
                        m, den, acc = carry
                        rows = pl.ds(pl.multiple_of(j * fb, fb), fb)
                        s = tdot(k_ref[rows, :], qb) * scale
                        if masked:
                            kp = lax.broadcasted_iota(jnp.int32, (fb, fb), 0) + j * fb
                            qp = lax.broadcasted_iota(jnp.int32, (fb, fb), 1) + i * fb
                            s = jnp.where(kp <= qp, s, NEG)
                        mn = jnp.maximum(m, jnp.max(s, axis=0, keepdims=True))
                        al = jnp.exp2(m - mn)
                        p = jnp.exp2(s - mn)
                        return (mn, den * al + jnp.sum(p, axis=0, keepdims=True),
                                acc * al + vdot(v_ref[rows, :], p.astype(BF16)))

                    return step

                st = (jnp.full((1, fb), NEG, F32), jnp.zeros((1, fb), F32), jnp.zeros((d, fb), F32))
                for a in range(2):
                    st = lax.fori_loop(0, c // fb, kstep(ks[a], vs[a], False), st)
                own = i + 1 if causal else f_ref[0] * (n // fb)
                st = lax.fori_loop(0, own, kstep(ks[2], vs[2], causal), st)
                st = lax.fori_loop(0, f_ref[1 if causal else 0] * (n // fb), kstep(ks[3], vs[3], False), st)
                finish(st[1], st[2], st[0], qs)
                return 0

            lax.fori_loop(0, tq // fb, qblock, 0)

    kspec = lambda rows: pl.BlockSpec((rows, d), lambda h, f: (0, h + h0))
    rows = [c, c, n, n]
    keys = 2 * c + n
    return pl.pallas_call(
        kern,
        grid_spec=pltpu.PrefetchScalarGridSpec(
            num_scalar_prefetch=1,
            grid=(nh,),
            in_specs=[pl.BlockSpec((tq, d), lambda h, f: (0, h + qcol))] + [kspec(r) for r in rows] * 2,
            out_specs=[pl.BlockSpec((d, tq), lambda h, f: (h, 0)), pl.BlockSpec((1, 1, tq), lambda h, f: (h, 0, 0))],
            scratch_shapes=[pltpu.VMEM((d, tq), F32), pltpu.VMEM((8, tq), F32)],
        ),
        out_shape=[jax.ShapeDtypeStruct((nh * d, tq), F32), jax.ShapeDtypeStruct((nh, 1, tq), F32)],
        compiler_params=pltpu.CompilerParams(vmem_limit_bytes=VMEM),
        cost_estimate=pl.CostEstimate(flops=12 * tq * keys * nh * d, bytes_accessed=4 * keys * nh * d,
                                      transcendentals=tq * keys * nh),
    )(flags, q, *[kv[0] for kv in kvs], *[kv[1] for kv in kvs])


def _merge(loc, first, rem, nh, d):
    tq = loc[0].shape[1]
    sizes = [l.shape[0] for _, l in rem]
    starts = [sum(sizes[:i]) for i in range(len(sizes))]

    def kern(o1_ref, l1_ref, *refs):
        o_ref = refs[-1]
        h = pl.program_id(0)

        def one(o2_ref, l2_ref):
            a, b = l1_ref[0], l2_ref[0]
            m = jnp.maximum(a, b)
            wa, wb = jnp.exp2(a - m), jnp.exp2(b - m)
            t = 1.0 / (wa + wb)
            o_ref[...] = (o1_ref[...] * (wa * t) + o2_ref[...] * (wb * t)).astype(BF16).T

        for i, (s, n) in enumerate(zip(starts, sizes)):
            pl.when((h >= s) & (h < s + n))(functools.partial(one, refs[2 * i], refs[2 * i + 1]))

    in_specs = [pl.BlockSpec((d, tq), lambda h: (h + first, 0)), pl.BlockSpec((1, 1, tq), lambda h: (h + first, 0, 0))]
    for s, n in zip(starts, sizes):
        at = lambda h, s=s, n=n: jnp.clip(h - s, 0, n - 1)
        in_specs += [pl.BlockSpec((d, tq), lambda h, at=at: (at(h), 0)),
                     pl.BlockSpec((1, 1, tq), lambda h, at=at: (at(h), 0, 0))]
    return pl.pallas_call(
        kern,
        grid=(nh,),
        in_specs=in_specs,
        out_specs=pl.BlockSpec((tq, d), lambda h: (0, h)),
        out_shape=jax.ShapeDtypeStruct((tq, nh * d), BF16),
        compiler_params=pltpu.CompilerParams(vmem_limit_bytes=VMEM),
        cost_estimate=pl.CostEstimate(flops=2000 * tq * nh * d, bytes_accessed=10 * tq * nh * d, transcendentals=0),
    )(*loc, *[a for r in rem for a in r])


def _flatten(a, b, br=256):
    n, h, d = a.shape

    def kern(a_ref, b_ref, oa_ref, ob_ref):
        oa_ref[...] = a_ref[...].reshape(br, h * d)
        ob_ref[...] = b_ref[...].reshape(br, h * d)

    return pl.pallas_call(
        kern,
        grid=(n // br,),
        in_specs=[pl.BlockSpec((br, h, d), lambda i: (i, 0, 0))] * 2,
        out_specs=[pl.BlockSpec((br, h * d), lambda i: (i, 0))] * 2,
        out_shape=[jax.ShapeDtypeStruct((n, h * d), BF16)] * 2,
        compiler_params=pltpu.CompilerParams(vmem_limit_bytes=VMEM),
        cost_estimate=pl.CostEstimate(flops=1000 * n * h * d, bytes_accessed=8 * n * h * d, transcendentals=0),
    )(a, b)


def _out(t, terms, acc, ncols, final, bn=512):
    tl = terms[0][0].shape[0]
    nt = len(terms)

    def kern(t_ref, *refs):
        o_ref = refs[-1]
        r = None if acc is None else refs[2 * nt][...]
        for i in range(nt):
            p = jnp.dot(refs[i][...], refs[nt + i][...], preferred_element_type=F32)
            r = p if r is None else r + p
        o_ref[...] = r.astype(o_ref.dtype)

    nb = ncols // bn

    def wspec(o, row, mine):
        rows = o.shape[1]
        if mine:
            return pl.BlockSpec((rows, bn), lambda j, tt: (row // rows, j + tt[0] * nb))
        return pl.BlockSpec((rows, bn), lambda j, tt: (row // rows, j))

    ospec = pl.BlockSpec((tl, bn), lambda j, tt: (0, j))
    k = sum(o.shape[1] for o, *_ in terms)
    return pl.pallas_call(
        kern,
        grid_spec=pltpu.PrefetchScalarGridSpec(
            num_scalar_prefetch=1,
            grid=(nb,),
            in_specs=[pl.BlockSpec(o.shape, lambda j, tt: (0, 0)) for o, *_ in terms]
            + [wspec(o, row, mine) for o, _, row, mine in terms] + ([] if acc is None else [ospec]),
            out_specs=ospec,
        ),
        out_shape=jax.ShapeDtypeStruct((tl, ncols), BF16 if final else F32),
        compiler_params=pltpu.CompilerParams(vmem_limit_bytes=VMEM),
        cost_estimate=pl.CostEstimate(flops=2 * tl * k * ncols, bytes_accessed=2 * k * ncols, transcendentals=0),
    )(t, *[o for o, *_ in terms], *[w for _, w, *_ in terms], *([] if acc is None else [acc]))


def solution(mesh):
    ncp = mesh.shape['cp']
    ntp = mesh.shape['tp']
    row = P(('dp', 'cp'), None)
    cache = P(('dp', 'cp'), 'tp', None)
    col = P(None, 'tp')
    half = ncp // 2
    core = [(i, i ^ 1) for i in range(ncp)]
    chip = [(i, (i + half) % ncp) for i in range(ncp)]
    swap = [(0, 1), (1, 0)]

    def body(x, kc, vc, wq, wk, wv, wo):
        tl = x.shape[0]
        cl, hl, d = kc.shape
        w = hl * d
        r = lax.axis_index('cp')
        t = lax.axis_index('tp')
        flags = jnp.stack([(r < half).astype(jnp.int32), r % 2])
        tt = t.reshape(1)
        ncols = wo.shape[1] // ntp
        hq = hl // 2

        tabs = _tables(cl * ncp + r * tl + jnp.arange(tl, dtype=jnp.int32), d)
        qs, qr = [], []
        prev = tabs[0]
        for i in range(2):
            qs.append(_proj(x, _after(wq, prev), tabs, i * (w // 2), w // 2, d))
            prev = qs[i]
            qr.append(lax.ppermute(prev, 'cp', chip))
        kc2, vc2 = _flatten(_after(kc, prev), vc)
        kcp = lax.ppermute(kc2, 'cp', core)
        vcp = lax.ppermute(vc2, 'cp', core)
        k = _proj(x, _after(wk, vc2), tabs, 0, w, d)
        kp = lax.ppermute(k, 'cp', core)
        v = _proj(x, _after(wv, k), None, 0, w, d)
        vp = lax.ppermute(v, 'cp', core)
        wo_other = lax.ppermute(lax.dynamic_slice(_after(wo, v), (0, (1 - t) * ncols), (w, ncols)), 'tp', swap)
        kvs = [(kc2, vc2), (kcp, vcp), (k, v), (kp, vp)]

        prev, y = v, None
        rem, loc, os = {}, {}, {}
        for kind, h0, nh in ORDER:
            if kind == 'R':
                o, l = _attend(_after(flags, prev), qr[h0 // hq], h0 % hq, kvs, h0, nh, d, False)
                prev = l
            elif kind == 'L':
                loc[h0, nh] = _attend(_after(flags, prev), qs[h0 // hq], h0 % hq, kvs, h0, nh, d, True)
                prev = loc[h0, nh][1]
            elif kind == 'M':
                (l0, ln), part = next((k, p) for k, p in loc.items() if k[0] <= h0 < sum(k))
                prev = _merge((part[0], _after(part[1], prev)), h0 - l0,
                              [rem[g] for g in sorted(rem) if h0 <= g < h0 + nh], nh, d)
                os[h0] = [(prev, wo, h0 * d, True)]
            else:
                terms = sum([os[g] for g in sorted(os) if h0 <= g < h0 + nh], [])
                prev = y = _out(_after(tt, prev), terms, y, ncols, kind == 'Z')
            if kind == 'R':
                rem[h0] = lax.ppermute(o, 'cp', chip), lax.ppermute(l, 'cp', chip)
            elif kind == 'M':
                os[h0].append((lax.ppermute(prev, 'tp', swap), wo_other, h0 * d, False))
        return y, k.reshape(tl, hl, d), v.reshape(tl, hl, d)

    return jax.shard_map(body, mesh=mesh,
                         in_specs=(row, cache, cache, col, col, col, P('tp', None)),
                         out_specs=(P(('dp', 'cp'), 'tp'), cache, cache), check_vma=False)
```

time: 1410 us -> 501 us (0.36)
  the two profiles are of different devices: /device:TPU:0 before, /device:TPU:1 now
where the time goes in v1:
time: 501 us; the launch traced here: 493 us
  Pallas kernels  343 us (68%)
  waiting for transfers between devices  112 us (22%)
  local copies, waits for them, and re-layouts  21.2 us (4%)
  starting transfers between devices  11.7 us (2%)
    pallas_call x6, Pallas kernels, _attend(): pl.pallas_call(kern, grid_spec=pltpu.PrefetchScalarGridSpec(num_scalar_pr...  205 us
    pallas_call x4, Pallas kernels, _proj(): pl.pallas_call(kern, grid=(ncols // bn,), in_specs=[full((m, k)), pl.Bloc...  78 us
    ppermute x8, waiting for transfers between devices, body(): rem[h0] = (lax.ppermute(o, 'cp', chip), lax.ppermute(l, 'cp', chip))  75.5 us
    ppermute x2, waiting for transfers between devices, body(): qr.append(lax.ppermute(prev, 'cp', chip))  36.7 us
    pallas_call x2, Pallas kernels, _out(): pl.pallas_call(kern, grid_spec=pltpu.PrefetchScalarGridSpec(num_scalar_pr...  29.2 us
    pallas_call x3, Pallas kernels, _merge(): pl.pallas_call(kern, grid=(nh,), in_specs=in_specs, out_specs=pl.BlockSpe...  16.3 us
    pallas_call x1, Pallas kernels, _flatten(): pl.pallas_call(kern, grid=(n // br,), in_specs=[pl.BlockSpec((br, h, d),...  14.7 us
    unnamed x26, local copies, waits for them, and re-layouts  12.7 us
  transfers between devices with their start and end apart: 18, of which 4 were waited for; matrix products, arithmetic and copies ran while one was open for 4% of the time, Pallas kernels for 59%

profile of v1, /device:TPU:1, one launch (start us, length us, event | category | flops | bytes accessed | tf_op | source)
XLA Modules:
  0.0 492.8 jit_solution(5110640306827888387)
XLA Ops:
  3.9 14.9 %shard_map.94.q_ref = bf16[1024,1024]{1,0:T(8,128)(2,1)} custom-call(bf16[1024,4096]{1,0:T(8,128)(2,1)} %refs_0_.7, bf16[4096,2048]{1,0:T(8,128)(2,1)} %refs_1_.1, f32[1024,128]{1,0:T(8,128)} %get-tuple-element.68.refs_2_, f32[1024,128]{1,0:T(8,128)} %get-tuple-element.69.refs_3_), custom_call_target="tpu_custom_call" | custom-call | flops 8589934592 | bytes 18874368 | tf_op jit(solution)/shard_map/pallas_call | solution.py:52
  18.8 14.9 %shard_map.95.q_ref = bf16[1024,1024]{1,0:T(8,128)(2,1)} custom-call(bf16[1024,4096]{1,0:T(8,128)(2,1)} %refs_0_.7, bf16[4096,2048]{1,0:T(8,128)(2,1)} %refs_1_.1, f32[1024,128]{1,0:T(8,128)} %get-tuple-element.68.refs_2_, f32[1024,128]{1,0:T(8,128)} %get-tuple-element.69.refs_3_), custom_call_target="tpu_custom_call" | custom-call | flops 8589934592 | bytes 18874368 | tf_op jit(solution)/shard_map/pallas_call | solution.py:52
  33.6 14.7 %shard_map.96 = (bf16[2048,2048]{1,0:T(8,128)(2,1)}, bf16[2048,2048]{1,0:T(8,128)(2,1)}) custom-call(bf16[2048,16,128]{2,1,0:T(8,128)(2,1)} %a_ref, bf16[2048,16,128]{2,1,0:T(8,128)(2,1)} %b_ref.1), custom_call_target="tpu_custom_call" | custom-call | flops 4194304000 | bytes 33554432 | tf_op jit(solution)/shard_map/pallas_call | solution.py:223
  48.8 24.7 %shard_map.97.refs_2_ = bf16[1024,2048]{1,0:T(8,128)(2,1)} custom-call(bf16[1024,4096]{1,0:T(8,128)(2,1)} %refs_0_.7, bf16[4096,2048]{1,0:T(8,128)(2,1)} %refs_1_.2, f32[1024,128]{1,0:T(8,128)} %get-tuple-element.68.refs_2_, f32[1024,128]{1,0:T(8,128)} %get-tuple-element.69.refs_3_), custom_call_target="tpu_custom_call" | custom-call | flops 17179869184 | bytes 29360128 | tf_op jit(solution)/shard_map/pallas_call | solution.py:52
  73.5 23.6 %shard_map.98.refs_6_ = bf16[1024,2048]{1,0:T(8,128)(2,1)} custom-call(bf16[1024,4096]{1,0:T(8,128)(2,1)} %refs_0_.7, bf16[4096,2048]{1,0:T(8,128)(2,1)} %refs_1_.3), custom_call_target="tpu_custom_call" | custom-call | flops 17179869184 | bytes 29360128 | tf_op jit(solution)/shard_map/pallas_call | solution.py:52
  97.6 2.2 collective-permute-start
  100.4 8.4 %constant_dynamic-slice_fusion = bf16[2048,2048]{1,0:T(8,128)(2,1)} fusion(bf16[2048,4096]{1,0:T(8,128)(2,1)} %refs_2_.1, s32[]{:T(128)S(6)} %select_n.11), kind=kLoop, calls=%fused_computation.8 | loop fusion | bytes 16777220 | tf_op jit(solution)/shard_map/dynamic_slice | solution.py:307
  108.9 36.7 %collective-permute-done.q_ref = bf16[1024,1024]{1,0:T(8,128)(2,1)} collective-permute-done((bf16[1024,1024]{1,0:T(8,128)(2,1)}, bf16[1024,1024]{1,0:T(8,128)(2,1)}, u32[]{:S(2)}, u32[]{:S(2)}) %collective-permute-start) | collective-permute-done | bytes 2097184 | tf_op jit(solution)/shard_map/ppermute | solution.py:299
  148.0 26.5 %shard_map.99 = (f32[512,1024]{1,0:T(8,128)}, f32[4,1,1024]{2,1,0:T(1,128)}) custom-call(s32[2]{0:T(128)} %pad_add_fusion.f_ref, bf16[1024,1024]{1,0:T(8,128)(2,1)} %collective-permute-done.q_ref, bf16[2048,2048]{1,0:T(8,128)(2,1)} %get-tuple-element.41.refs_0_, bf16[2048,2048]{1,0:T(8,128)(2,1)} %collective-permute-done.1.refs_1_, ...), custom_call_target="tpu_custom_call" | custom-call | flops 32212254720 | bytes 10485760 | tf_op jit(solution)/shard_map/pallas_call | solution.py:165
  174.5 26.5 %shard_map.100 = (f32[512,1024]{1,0:T(8,128)}, f32[4,1,1024]{2,1,0:T(1,128)}) custom-call(s32[2]{0:T(128)} %pad_add_fusion.f_ref, bf16[1024,1024]{1,0:T(8,128)(2,1)} %collective-permute-done.q_ref, bf16[2048,2048]{1,0:T(8,128)(2,1)} %get-tuple-element.41.refs_0_, bf16[2048,2048]{1,0:T(8,128)(2,1)} %collective-permute-done.1.refs_1_, ...), custom_call_target="tpu_custom_call" | custom-call | flops 32212254720 | bytes 10485760 | tf_op jit(solution)/shard_map/pallas_call | solution.py:165
  202.4 49.4 %shard_map.101 = (f32[1024,1024]{1,0:T(8,128)}, f32[8,1,1024]{2,1,0:T(1,128)}) custom-call(s32[2]{0:T(128)} %pad_add_fusion.f_ref, bf16[1024,1024]{1,0:T(8,128)(2,1)} %shard_map.94.q_ref, bf16[2048,2048]{1,0:T(8,128)(2,1)} %get-tuple-element.41.refs_0_, bf16[2048,2048]{1,0:T(8,128)(2,1)} %collective-permute-done.1.refs_1_, ...), custom_call_target="tpu_custom_call" | custom-call | flops 64424509440 | bytes 20971520 | tf_op jit(solution)/shard_map/pallas_call | solution.py:165
  251.8 26.3 %shard_map.102 = (f32[512,1024]{1,0:T(8,128)}, f32[4,1,1024]{2,1,0:T(1,128)}) custom-call(s32[2]{0:T(128)} %pad_add_fusion.f_ref, bf16[1024,1024]{1,0:T(8,128)(2,1)} %collective-permute-done.5.q_ref, bf16[2048,2048]{1,0:T(8,128)(2,1)} %get-tuple-element.41.refs_0_, bf16[2048,2048]{1,0:T(8,128)(2,1)} %collective-permute-done.1.refs_1_, ...), custom_call_target="tpu_custom_call" | custom-call | flops 32212254720 | bytes 10485760 | tf_op jit(solution)/shard_map/pallas_call | solution.py:165
  279.6 26.7 %shard_map.103 = (f32[512,1024]{1,0:T(8,128)}, f32[4,1,1024]{2,1,0:T(1,128)}) custom-call(s32[2]{0:T(128)} %pad_add_fusion.f_ref, bf16[1024,1024]{1,0:T(8,128)(2,1)} %collective-permute-done.5.q_ref, bf16[2048,2048]{1,0:T(8,128)(2,1)} %get-tuple-element.41.refs_0_, bf16[2048,2048]{1,0:T(8,128)(2,1)} %collective-permute-done.1.refs_1_, ...), custom_call_target="tpu_custom_call" | custom-call | flops 32212254720 | bytes 10485760 | tf_op jit(solution)/shard_map/pallas_call | solution.py:165
  307.9 18.3 %collective-permute-done.8.refs_2_ = f32[512,1024]{1,0:T(8,128)S(1)} collective-permute-done((f32[512,1024]{1,0:T(8,128)}, f32[512,1024]{1,0:T(8,128)S(1)}, u32[]{:S(2)}, u32[]{:S(2)}) %collective-permute-start.8) | collective-permute-done | bytes 2097184 | tf_op jit(solution)/shard_map/ppermute | solution.py:328
  326.1 44.9 %collective-permute-done.6.refs_0_ = f32[512,1024]{1,0:T(8,128)} collective-permute-done((f32[512,1024]{1,0:T(8,128)}, f32[512,1024]{1,0:T(8,128)}, u32[]{:S(2)}, u32[]{:S(2)}) %collective-permute-start.6) | collective-permute-done | bytes 2097184 | tf_op jit(solution)/shard_map/ppermute | solution.py:328
  371.1 7.6 %shard_map.104.refs_0_ = bf16[1024,1024]{1,0:T(8,128)(2,1)} custom-call(f32[1024,1024]{1,0:T(8,128)} %get-tuple-element.46.o1_ref, f32[8,1,1024]{2,1,0:T(1,128)} %get-tuple-element.52.l1_ref, f32[512,1024]{1,0:T(8,128)} %collective-permute-done.6.refs_0_, f32[4,1,1024]{2,1,0:T(1,128)} %copy-done.5, f32[512,1024]{1,0:T(8,128)} %copy-done.2, ...), custom_call_target="tpu_custom_call" | custom-call | flops 2097152000 | bytes 10485760 | tf_op jit(solution)/shard_map/pallas_call | solution.py:205
  378.9 49.3 %shard_map.105 = (f32[1024,1024]{1,0:T(8,128)}, f32[8,1,1024]{2,1,0:T(1,128)}) custom-call(s32[2]{0:T(128)} %pad_add_fusion.f_ref, bf16[1024,1024]{1,0:T(8,128)(2,1)} %shard_map.95.q_ref, bf16[2048,2048]{1,0:T(8,128)(2,1)} %get-tuple-element.41.refs_0_, bf16[2048,2048]{1,0:T(8,128)(2,1)} %collective-permute-done.1.refs_1_, ...), custom_call_target="tpu_custom_call" | custom-call | flops 64424509440 | bytes 20971520 | tf_op jit(solution)/shard_map/pallas_call | solution.py:165
  428.8 4.4 shard_map.106.refs_2_
  434.5 5.8 %copy.11 = bf16[128,8,16,128]{3,2,1,0:T(8,128)(2,1)} copy(bf16[128,8,16,128]{3,1,2,0:T(8,128)(2,1)} %bitcast.8) | data formatting | bytes 8388608
  440.3 3.4 copy.10
  443.7 12.3 %collective-permute-done.13.refs_1_ = f32[4,1,1024]{2,1,0:T(1,128)S(1)} collective-permute-done((f32[4,1,1024]{2,1,0:T(1,128)S(1)}, f32[4,1,1024]{2,1,0:T(1,128)S(1)}, u32[]{:S(2)}, u32[]{:S(2)}) %collective-permute-start.13) | collective-permute-done | bytes 16416 | tf_op jit(solution)/shard_map/ppermute | solution.py:328
  456.6 4.2 shard_map.107.refs_0_
  463.4 19.2 %shard_map.108.refs_4_ = f32[1024,2048]{1,0:T(8,128)} custom-call(s32[1]{0:T(128)} %bitcast.t_ref, bf16[1024,1024]{1,0:T(8,128)(2,1)} %shard_map.104.refs_0_, bf16[1024,1024]{1,0:T(8,128)(2,1)} %copy-done.1, bf16[1024,512]{1,0:T(8,128)(2,1)} %shard_map.106.refs_2_, bf16[1024,512]{1,0:T(8,128)(2,1)} %copy-done.3, bf16[2048,4096]{1,0:T(8,128)(2,1)} %refs_2_.1, ...), custom_call_target="tpu_custom_call" | custom-call | flops 12884901888 | bytes 12582912 | tf_op jit(solution)/shard_map/pallas_call | solution.py:256
  482.6 10.0 %shard_map.109 = bf16[1024,2048]{1,0:T(8,128)(2,1)} custom-call(s32[1]{0:T(128)} %bitcast.t_ref, bf16[1024,512]{1,0:T(8,128)(2,1)} %shard_map.107.refs_0_, bf16[1024,512]{1,0:T(8,128)(2,1)} %collective-permute-done.17.refs_1_, bf16[2048,4096]{1,0:T(8,128)(2,1)} %refs_2_.1, bf16[2048,2048]{1,0:T(8,128)(2,1)} %collective-permute-done.16.refs_5_.refs_7_.refs_3_, ...), custom_call_target="tpu_custom_call" | custom-call | flops 4294967296 | bytes 4194304 | tf_op jit(solution)/shard_map/pallas_call | solution.py:256
  (60 shorter events, 17.0 us)
Async XLA Ops:
  48.3 99.7 %collective-permute-start.3 = (bf16[2048,2048]{1,0:T(8,128)(2,1)}, bf16[2048,2048]{1,0:T(8,128)(2,1)}, u32[]{:S(2)}, u32[]{:S(2)}) collective-permute-start(bf16[2048,2048]{1,0:T(8,128)(2,1)} %get-tuple-element.37.refs_4_), channel_id=1, source_target_pairs={{0,1},{1,0},{2,3},{3,2},{4,5},{5,4},{6,7},{7,6}} | collective-permute-start | bytes 25165832 | tf_op jit(solution)/shard_map/ppermute | solution.py:302
  48.3 99.7 %collective-permute-start.1 = (bf16[2048,2048]{1,0:T(8,128)(2,1)}, bf16[2048,2048]{1,0:T(8,128)(2,1)}, u32[]{:S(2)}, u32[]{:S(2)}) collective-permute-start(bf16[2048,2048]{1,0:T(8,128)(2,1)} %get-tuple-element.41.refs_0_), channel_id=1, source_target_pairs={{0,1},{1,0},{2,3},{3,2},{4,5},{5,4},{6,7},{7,6}} | collective-permute-start | bytes 25165832 | tf_op jit(solution)/shard_map/ppermute | solution.py:301
  97.1 49.7 %collective-permute-start.4 = (bf16[1024,2048]{1,0:T(8,128)(2,1)}, bf16[1024,2048]{1,0:T(8,128)(2,1)}, u32[]{:S(2)}, u32[]{:S(2)}) collective-permute-start(bf16[1024,2048]{1,0:T(8,128)(2,1)} %shard_map.98.refs_6_), channel_id=1, source_target_pairs={{0,1},{1,0},{2,3},{3,2},{4,5},{5,4},{6,7},{7,6}} | collective-permute-start | bytes 12582920 | tf_op jit(solution)/shard_map/ppermute | solution.py:306
  97.1 51.0 %collective-permute-start.2 = (bf16[1024,2048]{1,0:T(8,128)(2,1)}, bf16[1024,2048]{1,0:T(8,128)(2,1)}, u32[]{:S(2)}, u32[]{:S(2)}) collective-permute-start(bf16[1024,2048]{1,0:T(8,128)(2,1)} %shard_map.97.refs_2_), channel_id=1, source_target_pairs={{0,1},{1,0},{2,3},{3,2},{4,5},{5,4},{6,7},{7,6}} | collective-permute-start | bytes 12582920 | tf_op jit(solution)/shard_map/ppermute | solution.py:304
  97.6 48.0 %collective-permute-start = (bf16[1024,1024]{1,0:T(8,128)(2,1)}, bf16[1024,1024]{1,0:T(8,128)(2,1)}, u32[]{:S(2)}, u32[]{:S(2)}) collective-permute-start(bf16[1024,1024]{1,0:T(8,128)(2,1)} %shard_map.94.q_ref), channel_id=1, source_target_pairs={{0,2},{1,3},{2,0},{3,1},{4,6},{5,7},{6,4},{7,5}} | collective-permute-start | bytes 6291464 | tf_op jit(solution)/shard_map/ppermute | solution.py:299
  100.4 45.2 %copy-start.8 = (bf16[1024,1024]{1,0:T(8,128)(2,1)S(1)}, bf16[1024,1024]{1,0:T(8,128)(2,1)}, u32[]{:S(2)}) copy-start(bf16[1024,1024]{1,0:T(8,128)(2,1)} %shard_map.95.q_ref) | copy-start | bytes 6291460
  145.6 106.2 %collective-permute-start.5 = (bf16[1024,1024]{1,0:T(8,128)(2,1)S(1)}, bf16[1024,1024]{1,0:T(8,128)(2,1)}, u32[]{:S(2)}, u32[]{:S(2)}) collective-permute-start(bf16[1024,1024]{1,0:T(8,128)(2,1)S(1)} %copy-done.8), channel_id=1, source_target_pairs={{0,2},{1,3},{2,0},{3,1},{4,6},{5,7},{6,4},{7,5}} | collective-permute-start | bytes 6291464 | tf_op jit(solution)/shard_map/ppermute | solution.py:299
  146.8 314.3 %collective-permute-start.16 = (bf16[2048,2048]{1,0:T(8,128)(2,1)}, bf16[2048,2048]{1,0:T(8,128)(2,1)}, u32[]{:S(2)}, u32[]{:S(2)}) collective-permute-start(bf16[2048,2048]{1,0:T(8,128)(2,1)} %constant_dynamic-slice_fusion), channel_id=1, source_target_pairs={{0,4},{4,0},{1,5},{5,1},{2,6},{6,2},{3,7},{7,3}} | collective-permute-start | bytes 25165832 | tf_op jit(solution)/shard_map/ppermute | solution.py:307
  174.5 26.5 %copy-start.11 = (f32[4,1,1024]{2,1,0:T(1,128)S(1)}, f32[4,1,1024]{2,1,0:T(1,128)}, u32[]{:S(2)}) copy-start(f32[4,1,1024]{2,1,0:T(1,128)} %get-tuple-element.42) | copy-start | bytes 49156
  201.0 105.4 %collective-permute-start.9 = (f32[4,1,1024]{2,1,0:T(1,128)}, f32[4,1,1024]{2,1,0:T(1,128)S(1)}, u32[]{:S(2)}, u32[]{:S(2)}) collective-permute-start(f32[4,1,1024]{2,1,0:T(1,128)} %get-tuple-element.44), channel_id=1, source_target_pairs={{0,2},{1,3},{2,0},{3,1},{4,6},{5,7},{6,4},{7,5}} | collective-permute-start | bytes 49160 | tf_op jit(solution)/shard_map/ppermute | solution.py:328
  201.0 105.4 %collective-permute-start.7 = (f32[4,1,1024]{2,1,0:T(1,128)S(1)}, f32[4,1,1024]{2,1,0:T(1,128)S(1)}, u32[]{:S(2)}, u32[]{:S(2)}) collective-permute-start(f32[4,1,1024]{2,1,0:T(1,128)S(1)} %copy-done.11), channel_id=1, source_target_pairs={{0,2},{1,3},{2,0},{3,1},{4,6},{5,7},{6,4},{7,5}} | collective-permute-start | bytes 49160 | tf_op jit(solution)/shard_map/ppermute | solution.py:328
  278.2 48.0 %collective-permute-start.8 = (f32[512,1024]{1,0:T(8,128)}, f32[512,1024]{1,0:T(8,128)S(1)}, u32[]{:S(2)}, u32[]{:S(2)}) collective-permute-start(f32[512,1024]{1,0:T(8,128)} %get-tuple-element.54), channel_id=1, source_target_pairs={{0,2},{1,3},{2,0},{3,1},{4,6},{5,7},{6,4},{7,5}} | collective-permute-start | bytes 6291464 | tf_op jit(solution)/shard_map/ppermute | solution.py:328
  278.2 28.2 %copy-start.10 = (f32[4,1,1024]{2,1,0:T(1,128)S(1)}, f32[4,1,1024]{2,1,0:T(1,128)}, u32[]{:S(2)}) copy-start(f32[4,1,1024]{2,1,0:T(1,128)} %get-tuple-element.49) | copy-start | bytes 49156
  278.2 92.9 %collective-permute-start.6 = (f32[512,1024]{1,0:T(8,128)}, f32[512,1024]{1,0:T(8,128)}, u32[]{:S(2)}, u32[]{:S(2)}) collective-permute-start(f32[512,1024]{1,0:T(8,128)} %get-tuple-element.53), channel_id=1, source_target_pairs={{0,2},{1,3},{2,0},{3,1},{4,6},{5,7},{6,4},{7,5}} | collective-permute-start | bytes 6291464 | tf_op jit(solution)/shard_map/ppermute | solution.py:328
  306.4 64.7 %copy-start.4 = (f32[4,1,1024]{2,1,0:T(1,128)}, f32[4,1,1024]{2,1,0:T(1,128)S(1)}, u32[]{:S(2)}) copy-start(f32[4,1,1024]{2,1,0:T(1,128)S(1)} %collective-permute-done.9.refs_3_) | copy-start | bytes 49156
  306.4 121.8 %collective-permute-start.11 = (f32[4,1,1024]{2,1,0:T(1,128)S(1)}, f32[4,1,1024]{2,1,0:T(1,128)S(1)}, u32[]{:S(2)}, u32[]{:S(2)}) collective-permute-start(f32[4,1,1024]{2,1,0:T(1,128)S(1)} %copy-done.10), channel_id=1, source_target_pairs={{0,2},{1,3},{2,0},{3,1},{4,6},{5,7},{6,4},{7,5}} | collective-permute-start | bytes 49160 | tf_op jit(solution)/shard_map/ppermute | solution.py:328
  306.4 64.7 %copy-start.5 = (f32[4,1,1024]{2,1,0:T(1,128)}, f32[4,1,1024]{2,1,0:T(1,128)S(1)}, u32[]{:S(2)}) copy-start(f32[4,1,1024]{2,1,0:T(1,128)S(1)} %collective-permute-done.7.refs_1_) | copy-start | bytes 49156
  306.4 121.8 %collective-permute-start.10 = (f32[512,1024]{1,0:T(8,128)}, f32[512,1024]{1,0:T(8,128)}, u32[]{:S(2)}, u32[]{:S(2)}) collective-permute-start(f32[512,1024]{1,0:T(8,128)} %get-tuple-element.59), channel_id=1, source_target_pairs={{0,2},{1,3},{2,0},{3,1},{4,6},{5,7},{6,4},{7,5}} | collective-permute-start | bytes 6291464 | tf_op jit(solution)/shard_map/ppermute | solution.py:328
  326.1 44.9 %copy-start.2 = (f32[512,1024]{1,0:T(8,128)}, f32[512,1024]{1,0:T(8,128)S(1)}, u32[]{:S(2)}) copy-start(f32[512,1024]{1,0:T(8,128)S(1)} %collective-permute-done.8.refs_2_) | copy-start | bytes 6291460
  326.1 129.8 %collective-permute-start.12 = (f32[512,1024]{1,0:T(8,128)}, f32[512,1024]{1,0:T(8,128)}, u32[]{:S(2)}, u32[]{:S(2)}) collective-permute-start(f32[512,1024]{1,0:T(8,128)} %get-tuple-element.61), channel_id=1, source_target_pairs={{0,2},{1,3},{2,0},{3,1},{4,6},{5,7},{6,4},{7,5}} | collective-permute-start | bytes 6291464 | tf_op jit(solution)/shard_map/ppermute | solution.py:328
  378.6 82.4 %collective-permute-start.14 = (bf16[1024,1024]{1,0:T(8,128)(2,1)}, bf16[1024,1024]{1,0:T(8,128)(2,1)S(1)}, u32[]{:S(2)}, u32[]{:S(2)}) collective-permute-start(bf16[1024,1024]{1,0:T(8,128)(2,1)} %shard_map.104.refs_0_), channel_id=1, source_target_pairs={{0,4},{4,0},{1,5},{5,1},{2,6},{6,2},{3,7},{7,3}} | collective-permute-start | bytes 6291464 | tf_op jit(solution)/shard_map/ppermute | solution.py:330
  433.3 27.8 %collective-permute-start.15 = (bf16[1024,512]{1,0:T(8,128)(2,1)}, bf16[1024,512]{1,0:T(8,128)(2,1)S(1)}, u32[]{:S(2)}, u32[]{:S(2)}) collective-permute-start(bf16[1024,512]{1,0:T(8,128)(2,1)} %shard_map.106.refs_2_), channel_id=1, source_target_pairs={{0,4},{4,0},{1,5},{5,1},{2,6},{6,2},{3,7},{7,3}} | collective-permute-start | bytes 3145736 | tf_op jit(solution)/shard_map/ppermute | solution.py:330
  434.5 21.5 %collective-permute-start.13 = (f32[4,1,1024]{2,1,0:T(1,128)S(1)}, f32[4,1,1024]{2,1,0:T(1,128)S(1)}, u32[]{:S(2)}, u32[]{:S(2)}) collective-permute-start(f32[4,1,1024]{2,1,0:T(1,128)S(1)} %copy-done.9), channel_id=1, source_target_pairs={{0,2},{1,3},{2,0},{3,1},{4,6},{5,7},{6,4},{7,5}} | collective-permute-start | bytes 49160 | tf_op jit(solution)/shard_map/ppermute | solution.py:328
  460.8 21.7 %collective-permute-start.17 = (bf16[1024,512]{1,0:T(8,128)(2,1)}, bf16[1024,512]{1,0:T(8,128)(2,1)}, u32[]{:S(2)}, u32[]{:S(2)}) collective-permute-start(bf16[1024,512]{1,0:T(8,128)(2,1)} %shard_map.107.refs_0_), channel_id=1, source_target_pairs={{0,4},{4,0},{1,5},{5,1},{2,6},{6,2},{3,7},{7,3}} | collective-permute-start | bytes 3145736 | tf_op jit(solution)/shard_map/ppermute | solution.py:330
  (6 other events, 15.7 us)
